TPU v7x, 512 devices: a whole 4x4x16 slice. The times are simulated.
512 devices in a mesh: unit: 2 (over core), zero: 16 (over z), model: 16 (over y, x).
Axes of the slice: x: 4, y: 4, z: 16, core: 2. Of those that a mesh axis runs over, the one named last changes fastest.
Arguments:
- first_query: float32 [16384, 8192], P(('unit', 'zero'), 'model'), parts along dimension 0, may hold values from -0.09375 to 0.09375
- second_query: float32 [16384, 8192], P(('unit', 'zero'), 'model'), parts along dimension 0, may hold values from -0.0625 to 0.0625
- first_key: float32 [16384, 1024], P(('unit', 'zero'), 'model'), parts along dimension 0, may hold values from -0.09375 to 0.09375
- second_key: float32 [16384, 1024], P(('unit', 'zero'), 'model'), parts along dimension 0, may hold values from -0.0625 to 0.0625
- first_value: float32 [16384, 1024], P(('unit', 'zero'), 'model'), parts along dimension 0, may hold values from -0.09375 to 0.09375
- second_value: float32 [16384, 1024], P(('unit', 'zero'), 'model'), parts along dimension 0, may hold values from -0.0625 to 0.0625
- mix_share: float32 [16384], P(('unit', 'zero')), parts along dimension 0, may hold values from 0.2 to 0.8
- norm_train: float32 [16384], P(('unit', 'zero', 'model')), parts along dimension 0, may hold values from 0.25 to 1.75
- norm_step: float32 [16384], P(('unit', 'zero', 'model')), parts along dimension 0, may hold values from -0.3 to 0.3
Outputs:
- serve_query: bfloat16 [16384, 8192], P('unit', 'model'), parts along dimension 0
- serve_key: bfloat16 [16384, 1024], P('unit', 'model'), parts along dimension 0
- serve_value: bfloat16 [16384, 1024], P('unit', 'model'), parts along dimension 0
- factor_query: float32 [16384], P(('unit', 'model')), parts along dimension 0
- factor_key: float32 [2048], P(('unit', 'model')), parts along dimension 0
- factor_value: float32 [2048], P(('unit', 'model')), parts along dimension 0
- serve_norm: bfloat16 [16384], P('unit'), parts along dimension 0
There are 2 independent parts, one for each index of `unit`. A program takes and returns all parts, laid end to end along the dimension named above; each array names one. Nothing has to cross between parts.
All inputs are finite; a program needn't handle non-finite values.
Results may differ from a plain program's by a relative error of at most 0.0004.
Values may be sent and summed in bfloat16 or wider, within the bound.
A program may use at most 128 MiB of HBM per device.

v0:
```python
import jax
import jax.numpy as jnp
from jax import lax
from jax.sharding import Mesh
from jax.sharding import PartitionSpec as P

ZERO_MODEL = ("zero", "model_0", "model_1")
MODEL = ("model_0", "model_1")
UNIT_ZERO_MODEL = ("unit", "zero", "model_0", "model_1")
UNIT_MODEL = ("unit", "model_0", "model_1")


def from_everyone(array, axis):
    length = lax.axis_size(axis)
    return lax.all_to_all(
        jnp.broadcast_to(array[None], (length, *array.shape)), axis, 0, 0, tiled=True
    )


def over_copies(array, axis):
    everything = from_everyone(array, axis)
    return jnp.sum(everything, axis=0)


def together(arrays, axis):
    ends = [0]
    for a in arrays:
        ends.append(ends[-1] + a.size)
    so_far = over_copies(jnp.concatenate([a.ravel() for a in arrays]), axis)
    return tuple((so_far[b:e].reshape(a.shape) for a, b, e in zip(arrays, ends, ends[1:])))


def side_by_side(arrays, axis, dim, along):
    widths = [a.shape[along] for a in arrays]
    both = jnp.concatenate(arrays, axis=along)
    filled = lax.all_gather(both, axis, axis=dim, tiled=True)
    return tuple(jnp.split(filled, [sum(widths[:k]) for k in range(1, len(widths))], axis=along))


def joined_along(blocks, dim):
    blocks = jnp.moveaxis(blocks, 0, dim)
    lengths = blocks.shape
    return blocks.reshape(*lengths[:dim], lengths[dim] * lengths[dim + 1], *lengths[dim + 2 :])


def all_blocks(array, axes, turns):
    blocks = array[None]
    for k in turns:
        blocks = lax.all_gather(blocks, axes[k], axis=0, tiled=True)
    block = [lax.axis_size(axes[k]) for k in reversed(turns)]
    blocks = blocks.reshape(*block, *array.shape)
    turned = sorted(range(len(turns)), key=lambda place: turns[len(turns) - 1 - place])
    return blocks.transpose(*turned, *range(len(turns), blocks.ndim)).reshape(-1, *array.shape)


def whole_of(array, axes, turns, dim):
    return joined_along(all_blocks(array, axes, turns), dim)


def on_device(
    first_query,
    second_query,
    first_key,
    second_key,
    first_value,
    second_value,
    mix_share,
    norm_train,
    norm_step,
):
    fresh_query = mix_share[:, None] * first_query + (1.0 - mix_share[:, None]) * second_query
    fresh_key = mix_share[:, None] * first_key + (1.0 - mix_share[:, None]) * second_key
    fresh_value = mix_share[:, None] * first_value + (1.0 - mix_share[:, None]) * second_value
    total_query, total_key, total_value = together(
        (
            jnp.sum(fresh_query * fresh_query, axis=0),
            jnp.sum(fresh_key * fresh_key, axis=0),
            jnp.sum(fresh_value * fresh_value, axis=0),
        ),
        "zero",
    )
    factor_query = jnp.sqrt(total_query)
    factor_key = jnp.sqrt(total_key)
    factor_value = jnp.sqrt(total_value)
    narrow_query, narrow_key, narrow_value = (
        (fresh_query / factor_query).astype(jnp.bfloat16),
        (fresh_key / factor_key).astype(jnp.bfloat16),
        (fresh_value / factor_value).astype(jnp.bfloat16),
    )
    serve_query, serve_key, serve_value = side_by_side(
        (narrow_query, narrow_key, narrow_value), "zero", 0, 1
    )
    serve_norm = whole_of((norm_train + norm_step).astype(jnp.bfloat16), ZERO_MODEL, (0, 1, 2), 0)
    return (serve_query, serve_key, serve_value, factor_query, factor_key, factor_value, serve_norm)


def solution(mesh):
    split = Mesh(
        mesh.devices.reshape(mesh.shape["unit"], mesh.shape["zero"], 4, 4),
        ("unit", "zero", "model_0", "model_1"),
    )
    return jax.shard_map(
        on_device,
        mesh=split,
        in_specs=(
            P(("unit", "zero"), MODEL),
            P(("unit", "zero"), MODEL),
            P(("unit", "zero"), MODEL),
            P(("unit", "zero"), MODEL),
            P(("unit", "zero"), MODEL),
            P(("unit", "zero"), MODEL),
            P(("unit", "zero")),
            P(UNIT_ZERO_MODEL),
            P(UNIT_ZERO_MODEL),
        ),
        out_specs=(
            P("unit", MODEL),
            P("unit", MODEL),
            P("unit", MODEL),
            P(UNIT_MODEL),
            P(UNIT_MODEL),
            P(UNIT_MODEL),
            P("unit"),
        ),
        check_vma=False,
    )
```

profile of v0, /device:TPU:1, one launch (start us, length us, event | category | flops | bytes accessed | tf_op | source)
XLA Modules:
  0.0 190.5 jit_solution(13624009099179398102)
XLA Ops:
  7.2 0.0 copy-start
  7.2 0.0 all-gather.4.cloned.1.call-start
  7.2 0.8 broadcast_subtract_fusion
  8.0 1.6 copy.43
  9.5 0.0 copy-done
  9.6 0.0 copy-start.5
  9.6 0.3 copy.44
  9.9 0.3 copy-done.5
  10.2 0.0 copy-start.1
  10.2 0.0 copy-start.2
  10.2 0.0 copy-start.3
  10.2 0.0 copy-start.4
  10.3 0.2 multiply_reduce_fusion
  10.5 0.6 copy-done.1
  11.1 0.1 copy-done.2
  11.2 0.1 copy-done.3
  11.3 0.1 copy-done.4
  11.3 0.1 multiply_reduce_fusion.2
  11.5 0.1 pad_maximum_fusion.1
  11.6 27.1 %all_to_all.6 = f32[16,1,640]{2,1,0:T(1,128)S(1)} all-to-all(f32[16,1,640]{2,1,0:T(1,128)S(1)} %broadcast_in_dim.4), channel_id=1, replica_groups=mesh['unit'=2,'zero'=16,'model_0'=4,'model_1'=4] {'zero'}, dimensions={0} | all-to-all | bytes 81920 | tf_op jit(solution)/shard_map/all_to_all | solution.py:15
  38.7 0.1 slice_sqrt_fusion.2
  38.8 0.0 copy-start.7
  38.8 0.0 copy-start.8
  38.8 0.0 copy-start.6
  38.8 0.2 divide_convert_fusion
  39.0 0.4 copy-done.6
  39.4 0.0 copy-done.7
  39.4 0.0 copy-done.8
  39.4 0.0 copy-start.9
  39.4 0.0 copy-start.10
  39.4 0.1 divide_convert_fusion.2
  39.5 0.9 pad_maximum_fusion
  40.4 0.0 all-gather.4.cloned.1.call-update
  40.4 1.3 dynamic-slice
  42.3 0.0 copy-done.9
  42.3 0.0 copy-done.10
  42.3 0.2 dynamic-update-slice
  42.6 23.4 %all-reduce = bf16[512]{0:T(512)(128)(2,1)S(1)} all-reduce(bf16[512]{0:T(512)(128)(2,1)S(1)} %dynamic-update-slice), channel_id=2, replica_groups=mesh['unit'=2,'zero'=16,'model_0'=4,'model_1'=4] {'zero'}, use_global_device_ids=true, to_apply=%add | all-reduce | flops 512 | bytes 2048
  66.0 0.1 reshape.30
  66.0 10.6 %all_gather.14 = bf16[64,32]{1,0:T(8,128)(2,1)S(1)} all-gather(bf16[16,32]{1,0:T(8,128)(2,1)S(1)} %reshape.30), channel_id=1, replica_groups=mesh['unit'=2,'zero'=16,'model_0'=4,'model_1'=4] {'model_0'}, dimensions={0}, use_global_device_ids=true | all-gather | bytes 5120 | tf_op jit(solution)/shard_map/all_gather | solution.py:49
  76.6 0.1 copy.46
  76.7 10.4 %all-gather.1 = bf16[4,64,32]{1,2,0:T(8,128)(2,1)S(1)} all-gather(bf16[1,64,32]{1,2,0:T(8,128)(2,1)S(1)} %copy.46), channel_id=1, replica_groups=mesh['unit'=2,'zero'=16,'model_0'=4,'model_1'=4] {'model_1'}, dimensions={0}, use_global_device_ids=true | all-gather | bytes 20480 | tf_op jit(solution)/shard_map/all_gather | solution.py:49
  87.1 0.1 copy.47
  87.2 0.1 copy.48
  87.3 0.7 reshape_reshape.3
  88.0 73.0 %all-gather.4.cloned.1.call-done = bf16[8192,640]{0,1:T(8,128)(2,1)} async-done(((bf16[512,640]{0,1:T(8,128)(2,1)}), bf16[8192,640]{0,1:T(8,128)(2,1)}) %all-gather.4.cloned.1.call-update) | async-done | bytes 10485776 | tf_op jit(solution)/shard_map/all_gather | solution.py:36
  161.0 7.7 %split.12 = bf16[8192,512]{0,1:T(8,128)(2,1)} slice(bf16[8192,640]{0,1:T(8,128)(2,1)} %all-gather.4.cloned.1.call-done), slice={[0:8192], [0:512]} | slice | bytes 16777216 | tf_op jit(solution)/shard_map/split | solution.py:37
  168.7 11.9 %copy.49 = bf16[8192,512]{1,0:T(8,128)(2,1)} copy(bf16[8192,512]{0,1:T(8,128)(2,1)} %split.12) | data formatting | bytes 16777216
  180.6 3.0 %fusion = (bf16[8192,64]{0,1:T(8,128)(2,1)}, bf16[8192,64]{0,1:T(8,128)(2,1)}) fusion(bf16[8192,640]{0,1:T(8,128)(2,1)} %all-gather.4.cloned.1.call-done), kind=kLoop, calls=%fused_computation.16 | loop fusion | bytes 4194304 | tf_op jit(solution)/shard_map/split | solution.py:37
  (5 shorter events, 0.1 us)
Async XLA Ops:
  7.2 2.4 %copy-start = (f32[512,512]{1,0:T(8,128)S(1)}, f32[512,512]{1,0:T(8,128)}, u32[]{:S(2)}) copy-start(f32[512,512]{1,0:T(8,128)} %param.10) | copy-start | bytes 3145732
  7.2 153.8 %all-gather.4.cloned.1.call-start = ((), (), s32[]{:S(2)}) async-start(), calls=%async_computation.1 | async-start | bytes 11141120 | tf_op jit(solution)/shard_map/all_gather | solution.py:36
  9.6 0.7 copy-start.5
  10.2 0.9 copy-start.1
  10.2 1.0 copy-start.2
  10.2 1.0 copy-start.3
  10.2 1.1 copy-start.4
  38.8 0.6 copy-start.7
  38.8 0.6 copy-start.8
  38.8 0.6 copy-start.6
  39.4 2.9 %copy-start.9 = (f32[32]{0:T(128)S(1)}, f32[32]{0:T(128)}, u32[]{:S(2)}) copy-start(f32[32]{0:T(128)} %param.16) | copy-start | bytes 388
  39.4 3.0 %copy-start.10 = (f32[32]{0:T(128)S(1)}, f32[32]{0:T(128)}, u32[]{:S(2)}) copy-start(f32[32]{0:T(128)} %param.17) | copy-start | bytes 388
Sparse Core Ops, SparseCore 0:
  40.5 120.4 all-gather.3
where the time goes:
time: 191 us
  waiting for transfers between devices  73 us (38%)
  blocking collectives  71.4 us (37%)
  local copies, waits for them, and re-layouts  28.8 us (15%)
  between operations  14.8 us (8%)
  other arithmetic  2.44 us (1%)
    all_gather x1, waiting for transfers between devices, side_by_side(): filled = lax.all_gather(both, axis, axis=dim, tiled=True)  73 us
    all_to_all x1, blocking collectives, from_everyone(): lax.all_to_all(jnp.broadcast_to(array[None], (length, *array.shape)), axi...  27.1 us
    unnamed x1, blocking collectives  23.4 us
    all_gather x2, blocking collectives, all_blocks(): blocks = lax.all_gather(blocks, axes[k], axis=0, tiled=True)  21 us
    unnamed x29, local copies, waits for them, and re-layouts  17 us
    split x2, local copies, waits for them, and re-layouts, side_by_side(): jnp.split(filled, [sum(widths[:k]) for k in range(1, len(widths))], axis=...  10.7 us
  transfers between devices with their start and end apart: 1, of which 1 were waited for; matrix products, arithmetic and copies ran while one was open for 1% of the time, Pallas kernels for 0%

commit v1 on v0

v1 whole, which is shorter than its diff:
```python
import functools

import jax
import jax.numpy as jnp
from jax import lax
from jax.experimental import pallas as pl
from jax.experimental.pallas import tpu as pltpu
from jax.sharding import PartitionSpec as P

MESH = pl.DeviceIdType.MESH
LANES = 128
PIECES = 10


def gather_kernel(
    first_q, second_q, first_k, second_k, first_v, second_v, mix, train, step,
    blocks, factors, norm,
    a_q, b_q, a_kv, b_kv, mix_row, share, norm_in, lane_row, fresh, stat, plane, norm_wide,
    load_sem, stat_send, stat_recv, plane_send, plane_recv,
    right_send, right_recv, left_send, left_recv,
):
    n, m = lax.axis_size("zero"), lax.axis_size("model")
    me, col = lax.axis_index("zero"), lax.axis_index("model")
    rows, cols = first_q.shape
    thin = first_k.shape[0]
    wide = rows + 2 * thin
    size = wide // PIECES
    half = PIECES // 2
    tiles = rows // LANES

    barrier = pltpu.get_barrier_semaphore()

    def greet_line(d, c):
        pl.semaphore_signal(barrier, inc=1, device_id={"zero": lax.rem(me + d, n)}, device_id_type=MESH)
        return c

    def greet_plane(d, c):
        pl.semaphore_signal(barrier, inc=1, device_id={"model": lax.rem(col + d, m)}, device_id_type=MESH)
        return c

    lax.fori_loop(1, n, greet_line, 0)
    lax.fori_loop(1, m, greet_plane, 0)

    loads = [pltpu.make_async_copy(mix, mix_row, load_sem.at[0])]
    for r in range(tiles):
        part = pl.ds(r * LANES, LANES)
        loads.append(pltpu.make_async_copy(first_q.at[part], a_q.at[part], load_sem.at[1 + 2 * r]))
        loads.append(pltpu.make_async_copy(second_q.at[part], b_q.at[part], load_sem.at[2 + 2 * r]))
    at = 1 + 2 * tiles
    for k, (src, dst) in enumerate(
        (
            (first_k, a_kv.at[pl.ds(0, thin)]),
            (first_v, a_kv.at[pl.ds(thin, thin)]),
            (second_k, b_kv.at[pl.ds(0, thin)]),
            (second_v, b_kv.at[pl.ds(thin, thin)]),
            (train, norm_in.at[0]),
            (step, norm_in.at[1]),
        )
    ):
        loads.append(pltpu.make_async_copy(src, dst, load_sem.at[at + k]))
    for load in loads:
        load.start()

    loads[0].wait()
    for r in range(tiles):
        row = mix_row[:, r * LANES : (r + 1) * LANES]
        share[r * LANES : (r + 1) * LANES, :] = jnp.broadcast_to(row, (LANES, LANES)).T

    sums = [jnp.zeros((8, LANES), jnp.float32) for _ in range(tiles)]
    for r in range(tiles):
        loads[1 + 2 * r].wait()
        loads[2 + 2 * r].wait()
        part = slice(r * LANES, (r + 1) * LANES)
        w = share[part, :]
        for c in range(tiles):
            lanes = slice(c * LANES, (c + 1) * LANES)
            f = w * a_q[part, lanes] + (1.0 - w) * b_q[part, lanes]
            fresh[part, lanes] = f
            sums[c] = sums[c] + jnp.sum((f * f).reshape(LANES // 8, 8, LANES), axis=0)
    for load in loads[at : at + 4]:
        load.wait()
    w = mix_row[...]
    f = w * a_kv[...] + (1.0 - w) * b_kv[...]
    fresh[rows:, :] = f
    s = f * f
    folded = s[:, :LANES]
    for c in range(1, tiles):
        folded = folded + s[:, c * LANES : (c + 1) * LANES]
    thin_sum = jnp.sum(folded.T, axis=0, keepdims=True)

    for load in loads[at + 4 :]:
        load.wait()
    gain = (norm_in[0] + norm_in[1]).astype(jnp.bfloat16).astype(jnp.float32)
    lane_row[...] = jnp.zeros_like(lane_row)
    share_of_row = gain.shape[1]
    per_row = LANES // share_of_row
    lane_row[0:1, 0:share_of_row] = gain
    gain = lane_row[...]
    spread = gain
    for k in range(1, per_row):
        spread = spread + pltpu.roll(gain, k * share_of_row, 1)
    lane = lax.broadcasted_iota(jnp.int32, (8, LANES), 1)
    spread = jnp.where(lane // share_of_row == lax.rem(col, per_row), spread, 0.0)

    row_at = lax.broadcasted_iota(jnp.int32, (8, LANES), 0)
    mine = jnp.zeros((8, LANES), jnp.float32)
    for c in range(tiles):
        mine = jnp.where(row_at == c, jnp.sum(sums[c], axis=0, keepdims=True), mine)
    mine = jnp.where(row_at == tiles, thin_sum, mine)
    mine = jnp.where(row_at == tiles + 1, spread[0:1, :], mine)
    stat[me] = mine

    pl.semaphore_wait(barrier, n - 1 + m - 1)

    def stat_copy(d):
        return pltpu.make_async_remote_copy(
            stat.at[me], stat.at[me], stat_send.at[d], stat_recv.at[me],
            device_id={"zero": lax.rem(me + d, n)}, device_id_type=MESH,
        )

    def stat_from(d):
        source = lax.rem(me + d, n)
        return pltpu.make_async_remote_copy(
            stat.at[source], stat.at[source], stat_send.at[d], stat_recv.at[source],
            device_id={"zero": source}, device_id_type=MESH,
        )

    def send_stat(d, c):
        stat_copy(d).start()
        return c

    def take_stat(d, c):
        stat_from(d).wait_recv()
        return c

    lax.fori_loop(1, n, send_stat, 0)
    lax.fori_loop(1, n, take_stat, 0)

    total = stat[0]
    for z in range(1, n):
        total = total + stat[z]
    factor = jnp.sqrt(total)
    factors[...] = factor
    inverse = 1.0 / factor
    thin_inverse = jnp.broadcast_to(inverse[tiles : tiles + 1, :], (LANES, LANES)).T

    def piece_copy(send, recv, origin, s, p, to):
        where = blocks.at[origin, pl.ds(p * size, size)]
        return pltpu.make_async_remote_copy(
            where, where, send.at[s * PIECES + p], recv.at[s * PIECES + p],
            device_id={"zero": to}, device_id_type=MESH,
        )

    after, before = lax.rem(me + 1, n), lax.rem(me + n - 1, n)

    def to_right(s, p):
        return piece_copy(right_send, right_recv, lax.rem(me + n - s, n), s, p, after)

    def to_left(s, p):
        return piece_copy(left_send, left_recv, lax.rem(me + s, n), s, p, before)

    def from_left(s, p):
        return piece_copy(right_send, right_recv, lax.rem(before + n - s, n), s, p, after)

    def from_right(s, p):
        return piece_copy(left_send, left_recv, lax.rem(after + s, n), s, p, before)

    for p in range(PIECES):
        low, high = p * size, (p + 1) * size
        edge = min(max(rows, low), high)
        if low < edge:
            for c in range(tiles):
                lanes = slice(c * LANES, (c + 1) * LANES)
                blocks[me, low:edge, lanes] = (fresh[low:edge, lanes] * inverse[c : c + 1, :]).astype(jnp.bfloat16)
        if edge < high:
            scale = thin_inverse[edge - rows : high - rows, :]
            for c in range(tiles):
                lanes = slice(c * LANES, (c + 1) * LANES)
                blocks[me, edge:high, lanes] = (fresh[edge:high, lanes] * scale).astype(jnp.bfloat16)
        to_right(0, p).start()
        to_left(0, p).start()

    plane[col] = stat[:, tiles + 1, :]

    def plane_copy(d):
        return pltpu.make_async_remote_copy(
            plane.at[col], plane.at[col], plane_send.at[d], plane_recv.at[col],
            device_id={"model": lax.rem(col + d, m)}, device_id_type=MESH,
        )

    def plane_from(d):
        source = lax.rem(col + d, m)
        return pltpu.make_async_remote_copy(
            plane.at[source], plane.at[source], plane_send.at[d], plane_recv.at[source],
            device_id={"model": source}, device_id_type=MESH,
        )

    def send_plane(d, c):
        plane_copy(d).start()
        return c

    def take_plane(d, c):
        plane_from(d).wait_recv()
        return c

    lax.fori_loop(1, m, send_plane, 0)

    last = n // 2 - 1

    def hop(s, c):
        def one(p, c):
            from_left(s - 1, p).wait_recv()
            to_right(s, p).start()
            from_right(s - 1, p).wait_recv()
            to_left(s, p).start()
            return c

        return lax.fori_loop(0, PIECES, one, c)

    lax.fori_loop(1, last, hop, 0)

    lax.fori_loop(1, m, take_plane, 0)
    per = m // per_row
    for k in range(per):
        line = plane[k * per_row]
        for j in range(1, per_row):
            line = line + plane[k * per_row + j]
        norm_wide[pl.ds(k, n, stride=per), :] = line
    norm[...] = norm_wide[...].astype(jnp.bfloat16)

    def near(p, c):
        from_left(last - 1, p).wait_recv()
        to_right(last, p).start()
        from_right(last - 1, p + half).wait_recv()
        to_left(last, p + half).start()
        return c

    def far(p, c):
        from_right(last - 1, p).wait_recv()
        from_left(last - 1, p + half).wait_recv()
        return c

    def end(p, c):
        from_left(last, p).wait_recv()
        from_right(last, p + half).wait_recv()
        return c

    lax.fori_loop(0, half, near, 0)
    lax.fori_loop(0, half, far, 0)
    lax.fori_loop(0, half, end, 0)

    def sent(s, c):
        def one(p, c):
            to_right(s, p).wait_send()
            to_left(s, p).wait_send()
            return c

        return lax.fori_loop(0, PIECES, one, c)

    def sent_last(p, c):
        to_right(last, p).wait_send()
        to_left(last, p + half).wait_send()
        return c

    def sent_small(d, c):
        stat_copy(d).wait_send()
        return c

    def sent_plane(d, c):
        plane_copy(d).wait_send()
        return c

    lax.fori_loop(0, last, sent, 0)
    lax.fori_loop(0, half, sent_last, 0)
    lax.fori_loop(1, n, sent_small, 0)
    lax.fori_loop(1, m, sent_plane, 0)


def place_kernel(n, rows, thin, blocks, factors, norm, query, key, value, f_query, f_key, f_value, norm_out, sems):
    copies = []
    for z in range(n):
        here = pl.ds(z * rows, rows)
        copies.append(pltpu.make_async_copy(blocks.at[z, pl.ds(0, rows)], query.at[here], sems.at[3 * z]))
        copies.append(pltpu.make_async_copy(blocks.at[z, pl.ds(rows, thin)], key.at[:, here], sems.at[3 * z + 1]))
        copies.append(pltpu.make_async_copy(blocks.at[z, pl.ds(rows + thin, thin)], value.at[:, here], sems.at[3 * z + 2]))
    for copy in copies:
        copy.start()
    tiles = f_query.shape[0]
    f_query[...] = factors[0:tiles, :]
    f_key[...] = factors[tiles : tiles + 1, 0:thin]
    f_value[...] = factors[tiles : tiles + 1, thin : 2 * thin]
    norm_out[...] = norm[...]
    for copy in copies:
        copy.wait()


def on_device(first_q, second_q, first_k, second_k, first_v, second_v, mix, train, step):
    n, m = lax.axis_size("zero"), lax.axis_size("model")
    rows, cols = first_q.shape
    thin = first_k.shape[1]
    wide = rows + 2 * thin
    piece = train.shape[0]
    tiles = rows // LANES
    f32, bf16 = jnp.float32, jnp.bfloat16
    anywhere = pl.BlockSpec(memory_space=pltpu.HBM)
    vmem = pl.BlockSpec(memory_space=pltpu.VMEM)
    dma = pltpu.SemaphoreType.DMA
    norm_rows = n * m * piece // LANES
    blocks, factors, norm = pl.pallas_call(
        gather_kernel,
        out_shape=(
            pltpu.VMEM((n, wide, cols), bf16),
            pltpu.VMEM((8, LANES), f32),
            pltpu.VMEM((norm_rows, LANES), bf16),
        ),
        in_specs=[anywhere] * 9,
        out_specs=(vmem, vmem, vmem),
        scratch_shapes=[
            pltpu.VMEM((rows, cols), f32),
            pltpu.VMEM((rows, cols), f32),
            pltpu.VMEM((2 * thin, rows), f32),
            pltpu.VMEM((2 * thin, rows), f32),
            pltpu.VMEM((1, rows), f32),
            pltpu.VMEM((rows, LANES), f32),
            pltpu.VMEM((2, 1, piece), f32),
            pltpu.VMEM((8, LANES), f32),
            pltpu.VMEM((wide, cols), f32),
            pltpu.VMEM((n, 8, LANES), f32),
            pltpu.VMEM((m, n, LANES), f32),
            pltpu.VMEM((norm_rows, LANES), f32),
            dma((1 + 2 * tiles + 6,)),
            dma((n,)),
            dma((n,)),
            dma((m,)),
            dma((m,)),
            dma((n // 2 * PIECES,)),
            dma((n // 2 * PIECES,)),
            dma((n // 2 * PIECES,)),
            dma((n // 2 * PIECES,)),
        ],
        compiler_params=pltpu.CompilerParams(
            collective_id=0, has_side_effects=True, vmem_limit_bytes=24 * 1024 * 1024
        ),
        name="gather",
    )(
        first_q, second_q, first_k.T, second_k.T, first_v.T, second_v.T,
        mix.reshape(1, rows), train.reshape(1, piece), step.reshape(1, piece),
    )
    query, key, value, f_query, f_key, f_value, norm = pl.pallas_call(
        functools.partial(place_kernel, n, rows, thin),
        out_shape=(
            jax.ShapeDtypeStruct((n * rows, cols), bf16),
            jax.ShapeDtypeStruct((thin, n * rows), bf16),
            jax.ShapeDtypeStruct((thin, n * rows), bf16),
            jax.ShapeDtypeStruct((tiles, LANES), f32),
            jax.ShapeDtypeStruct((1, thin), f32),
            jax.ShapeDtypeStruct((1, thin), f32),
            jax.ShapeDtypeStruct((norm_rows, LANES), bf16),
        ),
        in_specs=[vmem, vmem, vmem],
        out_specs=(anywhere, anywhere, anywhere, vmem, vmem, vmem, vmem),
        scratch_shapes=[dma((3 * n,))],
        compiler_params=pltpu.CompilerParams(vmem_limit_bytes=24 * 1024 * 1024),
        name="place",
    )(blocks, factors, norm)
    return (
        query, key.T, value.T,
        f_query.reshape(-1), f_key.reshape(-1), f_value.reshape(-1), norm.reshape(-1),
    )


def solution(mesh):
    own = P(("unit", "zero"), "model")
    return jax.shard_map(
        on_device,
        mesh=mesh,
        in_specs=(own, own, own, own, own, own, P(("unit", "zero")), P(("unit", "zero", "model")), P(("unit", "zero", "model"))),
        out_specs=(
            P("unit", "model"), P("unit", "model"), P("unit", "model"),
            P(("unit", "model")), P(("unit", "model")), P(("unit", "model")), P("unit"),
        ),
        check_vma=False,
    )
```

time: 191 us -> 146 us (0.76)
  Pallas kernels: 0 us -> 137 us
  waiting for transfers between devices: 73 us -> 0 us
  blocking collectives: 71.4 us -> 0 us
  local copies, waits for them, and re-layouts: 28.8 us -> 8.05 us
  between operations: 14.8 us -> 0.66 us
  other arithmetic: 2.44 us -> 0 us
    pallas_call x0 -> x2, Pallas kernels: none -> 137 us  [the longest x1 132 us: on_device(): pl.pallas_call(gather_kernel, out_shape=(pltpu.VMEM((n, wide, cols), bf16...]
    all_gather x1 -> x0, waiting for transfers between devices: 73 us -> none  [side_by_side(): filled = lax.all_gather(both, axis, axis=dim, tiled=True)]
    all_to_all x1 -> x0, blocking collectives: 27.1 us -> none  [from_everyone(): lax.all_to_all(jnp.broadcast_to(array[None], (length, *array.shape)), axi...]
    unnamed x1 -> x0, blocking collectives: 23.4 us -> none
    all_gather x2 -> x0, blocking collectives: 21 us -> none  [all_blocks(): blocks = lax.all_gather(blocks, axes[k], axis=0, tiled=True)]
    split x2 -> x0, local copies, waits for them, and re-layouts: 10.7 us -> none  [side_by_side(): jnp.split(filled, [sum(widths[:k]) for k in range(1, len(widths))], axis=...]
    unnamed x29 -> x18, local copies, waits for them, and re-layouts: 17 us -> 8.05 us
  transfers between devices with their start and end apart: 1 -> 0, of which waited for: 1 -> 0; matrix products, arithmetic and copies ran while one was open for 1% -> 0% of each run, Pallas kernels for 0% -> 0%
where the time goes in v1:
time: 146 us
  Pallas kernels  137 us (94%)
  local copies, waits for them, and re-layouts  8.05 us (6%)
    pallas_call x1, Pallas kernels, on_device(): pl.pallas_call(gather_kernel, out_shape=(pltpu.VMEM((n, wide, cols), bf16...  132 us
    unnamed x18, local copies, waits for them, and re-layouts  8.05 us
    pallas_call x1, Pallas kernels, on_device(): pl.pallas_call(functools.partial(place_kernel, n, rows, thin), out_shape=...  4.92 us

profile of v1, /device:TPU:1, one launch (start us, length us, event | category | flops | bytes accessed | tf_op | source)
XLA Modules:
  0.0 145.7 jit_solution(12758127717708188042)
XLA Ops:
  0.6 0.0 copy-start
  0.6 1.2 copy-done
  1.9 0.0 copy-start.1
  1.9 1.2 copy-done.1
  3.1 0.0 copy-start.2
  3.1 0.9 copy-done.2
  4.0 0.0 copy-start.3
  4.0 0.9 copy-done.3
  4.9 0.0 copy-start.4
  4.9 0.9 copy-done.4
  5.8 0.0 copy-start.5
  5.8 0.9 copy-done.5
  6.7 0.0 copy-start.6
  6.7 0.7 copy-done.6
  7.4 0.0 copy-start.7
  7.4 0.7 copy-done.7
  8.0 0.0 copy-start.8
  8.0 0.7 copy-done.8
  8.7 132.0 %gather.1 = (bf16[16,640,512]{2,1,0:T(8,128)(2,1)S(1)}, f32[8,128]{1,0:T(8,128)S(1)}, bf16[64,128]{1,0:T(8,128)(2,1)S(1)}) custom-call(f32[512,512]{1,0:T(8,128)S(1)} %copy-done, f32[512,512]{1,0:T(8,128)S(1)} %copy-done.1, f32[64,512]{1,0:T(8,128)S(1)} %bitcast.13, f32[64,512]{1,0:T(8,128)S(1)} %bitcast.14, f32[64,512]{1,0:T(8,128)S(1)} %bitcast.15, ...), custom_call_target="tpu_custom_call" | custom-call | tf_op jit(solution)/shard_map/gather/pallas_call | solution.py:309
  140.8 4.9 %place.1 = (bf16[8192,512]{1,0:T(8,128)(2,1)}, bf16[64,8192]{1,0:T(8,128)(2,1)}, bf16[64,8192]{1,0:T(8,128)(2,1)}, f32[4,128]{1,0:T(4,128)}, f32[1,64]{1,0:T(1,1...) custom-call(bf16[16,640,512]{2,1,0:T(8,128)(2,1)S(1)} %get-tuple-element.17.blocks, ...), custom_call_target="tpu_custom_call" | custom-call | tf_op jit(solution)/shard_map/place/pallas_call | solution.py:349
Async XLA Ops:
  0.6 1.2 copy-start
  1.9 1.2 copy-start.1
  3.1 0.9 copy-start.2
  4.0 0.9 copy-start.3
  4.9 0.9 copy-start.4
  5.8 0.9 copy-start.5
  6.7 0.7 copy-start.6
  7.4 0.7 copy-start.7
  8.0 0.7 copy-start.8

commit v2 on v1

v2 whole, which is shorter than its diff:
```python
import functools
import math

import jax
import jax.numpy as jnp
from jax import lax
from jax.experimental import pallas as pl
from jax.experimental.pallas import tpu as pltpu
from jax.sharding import PartitionSpec as P

MESH = pl.DeviceIdType.MESH
LANES = 128
PIECES = 8
EARLY = 1


def gather_kernel(
    first_q, second_q, first_k, second_k, first_v, second_v, mix, train, step,
    blocks, f_query, f_key, f_value, norm,
    a_q, b_q, a_kv, b_kv, mix_row, share, norm_in, lane_row, fresh, stat, gains, plane, norm_wide, early,
    load_sem, line_sem, plane_send, plane_recv, early_send, early_recv, sent_sem, right_recv, left_recv,
):
    n, m = lax.axis_size("zero"), lax.axis_size("model")
    me, col = lax.axis_index("zero"), lax.axis_index("model")
    rows, cols = first_q.shape
    thin = first_k.shape[0]
    wide = rows + 2 * thin
    size = wide // PIECES
    half = PIECES // 2
    tiles = rows // LANES
    side = math.isqrt(m)
    across, down = lax.rem(col, side), col // side

    def beside(d):
        return down * side + lax.rem(across + d, side)

    def below(d):
        return lax.rem(down + d, side) * side + across

    loads = [pltpu.make_async_copy(mix, mix_row, load_sem.at[0])]
    for r in range(tiles):
        part = pl.ds(r * LANES, LANES)
        loads.append(pltpu.make_async_copy(first_q.at[part], a_q.at[part], load_sem.at[1 + 2 * r]))
        loads.append(pltpu.make_async_copy(second_q.at[part], b_q.at[part], load_sem.at[2 + 2 * r]))
    at = 1 + 2 * tiles
    for k, (src, dst) in enumerate(
        (
            (first_k, a_kv.at[pl.ds(0, thin)]),
            (first_v, a_kv.at[pl.ds(thin, thin)]),
            (second_k, b_kv.at[pl.ds(0, thin)]),
            (second_v, b_kv.at[pl.ds(thin, thin)]),
            (train, norm_in.at[0]),
            (step, norm_in.at[1]),
        )
    ):
        loads.append(pltpu.make_async_copy(src, dst, load_sem.at[at + k]))
    for load in loads:
        load.start()

    barrier = pltpu.get_barrier_semaphore()

    def greet_line(d, c):
        pl.semaphore_signal(barrier, inc=1, device_id={"zero": lax.rem(me + d, n)}, device_id_type=MESH)
        return c

    lax.fori_loop(1, n, greet_line, 0)
    for peer in (beside(1), beside(side - 1), below(1), below(side - 1)):
        pl.semaphore_signal(barrier, inc=1, device_id={"model": peer}, device_id_type=MESH)

    loads[0].wait()
    for r in range(tiles):
        row = mix_row[:, r * LANES : (r + 1) * LANES]
        share[r * LANES : (r + 1) * LANES, :] = jnp.broadcast_to(row, (LANES, LANES)).T

    sums = [jnp.zeros((8, LANES), jnp.float32) for _ in range(tiles)]
    for r in range(tiles):
        loads[1 + 2 * r].wait()
        loads[2 + 2 * r].wait()
        part = slice(r * LANES, (r + 1) * LANES)
        w = share[part, :]
        for c in range(tiles):
            lanes = slice(c * LANES, (c + 1) * LANES)
            f = w * a_q[part, lanes] + (1.0 - w) * b_q[part, lanes]
            fresh[part, lanes] = f
            sums[c] = sums[c] + jnp.sum((f * f).reshape(LANES // 8, 8, LANES), axis=0)
    for load in loads[at : at + 4]:
        load.wait()
    w = mix_row[...]
    f = w * a_kv[...] + (1.0 - w) * b_kv[...]
    fresh[rows:, :] = f
    s = f * f
    folded = s[:, :LANES]
    for c in range(1, tiles):
        folded = folded + s[:, c * LANES : (c + 1) * LANES]
    thin_sum = jnp.sum(folded.T, axis=0, keepdims=True)

    for load in loads[at + 4 :]:
        load.wait()
    gain = (norm_in[0] + norm_in[1]).astype(jnp.bfloat16).astype(jnp.float32)
    lane_row[...] = jnp.zeros_like(lane_row)
    share_of_row = gain.shape[1]
    per_row = LANES // share_of_row
    lane_row[0:1, 0:share_of_row] = gain
    gain = lane_row[...]
    spread = gain
    for k in range(1, per_row):
        spread = spread + pltpu.roll(gain, k * share_of_row, 1)
    lane = lax.broadcasted_iota(jnp.int32, (8, LANES), 1)
    spread = jnp.where(lane // share_of_row == lax.rem(col, per_row), spread, 0.0)

    for c in range(tiles):
        stat[me, c] = jnp.sum(sums[c], axis=0, keepdims=True)
    stat[me, tiles] = thin_sum
    gains[me] = spread[0:1, :]

    pl.semaphore_wait(barrier, n - 1 + 4)

    def to_line(ref, k, d):
        return pltpu.make_async_remote_copy(
            ref.at[me], ref.at[me], line_sem.at[2 * k], line_sem.at[2 * k + 1],
            device_id={"zero": lax.rem(me + d, n)}, device_id_type=MESH,
        )

    def whole_line(ref, k):
        every = ref.at[pl.ds(0, n - 1)]
        return pltpu.make_async_remote_copy(
            every, every, line_sem.at[2 * k], line_sem.at[2 * k + 1],
            device_id={"zero": lax.rem(me + 1, n)}, device_id_type=MESH,
        )

    for k, ref in enumerate((stat, gains)):
        to_line(ref, k, n // 2).start()
        for d in range(1, n // 2):
            to_line(ref, k, n // 2 + d).start()
            to_line(ref, k, n // 2 - d).start()

    after, before = lax.rem(me + 1, n), lax.rem(me + n - 1, n)

    def early_copy(p, way):
        where = pl.ds(p * size, size)
        return pltpu.make_async_remote_copy(
            fresh.at[where], early.at[way, where], early_send.at[way * EARLY + p], early_recv.at[way * EARLY + p],
            device_id={"zero": (after, before)[way]}, device_id_type=MESH,
        )

    for p in range(EARLY):
        early_copy(p, 0).start()
        early_copy(p, 1).start()

    whole_line(stat, 0).wait_recv()

    inverse = []
    for c in range(tiles + 1):
        total = stat[0, c]
        for z in range(1, n):
            total = total + stat[z, c]
        factor = jnp.sqrt(total)
        inverse.append(1.0 / factor)
        if c < tiles:
            f_query[c : c + 1, :] = factor
        else:
            f_key[...] = factor[:, :thin]
            f_value[...] = factor[:, thin:]
    thin_inverse = jnp.broadcast_to(inverse[tiles], (LANES, LANES)).T

    def rounded(source, owner, p):
        base = pl.multiple_of(owner * wide, wide)
        low, high = p * size, (p + 1) * size
        edge = min(max(rows, low), high)
        if low < edge:
            for c in range(tiles):
                lanes = slice(c * LANES, (c + 1) * LANES)
                blocks[pl.ds(base + low, edge - low), lanes] = (source[low:edge, lanes] * inverse[c]).astype(jnp.bfloat16)
        if edge < high:
            scale = thin_inverse[edge - rows : high - rows, :]
            for c in range(tiles):
                lanes = slice(c * LANES, (c + 1) * LANES)
                blocks[pl.ds(base + edge, high - edge), lanes] = (source[edge:high, lanes] * scale).astype(jnp.bfloat16)

    def piece_copy(way, recv, origin, s, p, to):
        where = blocks.at[pl.ds(pl.multiple_of(origin * wide + p * size, size), size)]
        return pltpu.make_async_remote_copy(
            where, where, sent_sem.at[way], recv.at[s * PIECES + p],
            device_id={"zero": to}, device_id_type=MESH,
        )

    def to_right(s, p):
        return piece_copy(0, right_recv, lax.rem(me + n - s, n), s, p, after)

    def to_left(s, p):
        return piece_copy(1, left_recv, lax.rem(me + s, n), s, p, before)

    def from_left(s, p):
        return piece_copy(0, right_recv, lax.rem(before + n - s, n), s, p, after)

    def from_right(s, p):
        return piece_copy(1, left_recv, lax.rem(after + s, n), s, p, before)

    def both(s, p):
        to_right(s, p).start()
        to_left(s, p).start()

    for p in range(EARLY, PIECES):
        rounded(fresh, me, p)
        if p > EARLY:
            both(0, p - 1)
    for p in range(EARLY):
        rounded(fresh, me, p)
    both(0, PIECES - 1)
    for p in range(EARLY):
        early_copy(p, 0).wait_recv()
        rounded(early.at[0], before, p)
        if p:
            to_left(1, p - 1).start()
        early_copy(p, 1).wait_recv()
        rounded(early.at[1], after, p)
        to_right(1, p).start()

    whole_line(gains, 1).wait_recv()
    for z in range(n):
        plane[col, z : z + 1, :] = gains[z]
    if EARLY:
        to_left(1, EARLY - 1).start()

    def plane_copy(k):
        if k < side - 1:
            slot = plane.at[pl.ds(beside(side - k), 1)]
            to = beside(1)
        else:
            slot = plane.at[pl.ds(lax.rem(down + side - (k - side + 1), side) * side, side)]
            to = below(1)
        return pltpu.make_async_remote_copy(
            slot, slot, plane_send.at[k], plane_recv.at[k], device_id={"model": to}, device_id_type=MESH
        )

    def plane_from(k):
        if k < side - 1:
            slot = plane.at[pl.ds(beside(2 * side - 1 - k), 1)]
            to = beside(1)
        else:
            slot = plane.at[pl.ds(lax.rem(down + 2 * side - 1 - (k - side + 1), side) * side, side)]
            to = below(1)
        return pltpu.make_async_remote_copy(
            slot, slot, plane_send.at[k], plane_recv.at[k], device_id={"model": to}, device_id_type=MESH
        )

    last = n // 2 - 1
    turns = 2 * (side - 1)
    plane_copy(0).start()
    for s in range(1, last):

        def one(p, c):
            from_left(s - 1, p).wait_recv()
            to_right(s, p).start()
            from_right(s - 1, p).wait_recv()
            to_left(s, p).start()
            return c

        lax.fori_loop(EARLY if s == 1 else 0, PIECES, one, 0)
        if s <= turns:
            plane_from(s - 1).wait_recv()
            if s < turns:
                plane_copy(s).start()
    for k in range(max(last - 1, 0), turns):
        plane_from(k).wait_recv()
        if k + 1 < turns:
            plane_copy(k + 1).start()

    per = m // per_row
    for k in range(per):
        line = plane[k * per_row]
        for j in range(1, per_row):
            line = line + plane[k * per_row + j]
        norm_wide[pl.ds(k, n, stride=per), :] = line
    norm[...] = norm_wide[...].astype(jnp.bfloat16)

    def near(p, c):
        from_left(last - 1, p).wait_recv()
        to_right(last, p).start()
        from_right(last - 1, p + half).wait_recv()
        to_left(last, p + half).start()
        return c

    def far(p, c):
        from_right(last - 1, p).wait_recv()
        from_left(last - 1, p + half).wait_recv()
        return c

    def end(p, c):
        from_left(last, p).wait_recv()
        from_right(last, p + half).wait_recv()
        return c

    lax.fori_loop(0, half, near, 0)
    lax.fori_loop(0, half, far, 0)
    lax.fori_loop(0, half, end, 0)

    for p in range(EARLY):
        early_copy(p, 0).wait_send()
        early_copy(p, 1).wait_send()
    out = blocks.at[pl.ds(0, (last * PIECES - EARLY + half) * size)]
    for way, to in enumerate((after, before)):
        pltpu.make_async_remote_copy(
            out, out, sent_sem.at[way], right_recv.at[0], device_id={"zero": to}, device_id_type=MESH
        ).wait_send()
    whole_line(stat, 0).wait_send()
    whole_line(gains, 1).wait_send()
    for k in range(turns):
        plane_copy(k).wait_send()


def place_kernel(n, rows, thin, blocks, *refs):
    query, key, value = refs[4:7]
    sems = refs[-1]
    wide = rows + 2 * thin
    pairs = []
    for z in range(n):
        here = pl.ds(z * rows, rows)
        pairs.append((blocks.at[pl.ds(z * wide, rows)], query.at[here]))
        pairs.append((blocks.at[pl.ds(z * wide + rows, thin)], key.at[:, here]))
        pairs.append((blocks.at[pl.ds(z * wide + rows + thin, thin)], value.at[:, here]))
    pairs.extend(zip(refs[:4], refs[7:11]))
    copies = [pltpu.make_async_copy(src, dst, sems.at[k]) for k, (src, dst) in enumerate(pairs)]
    for copy in copies:
        copy.start()
    for copy in copies:
        copy.wait()


def on_device(first_q, second_q, first_k, second_k, first_v, second_v, mix, train, step):
    n, m = lax.axis_size("zero"), lax.axis_size("model")
    rows, cols = first_q.shape
    thin = first_k.shape[1]
    wide = rows + 2 * thin
    piece = train.shape[0]
    tiles = rows // LANES
    f32, bf16 = jnp.float32, jnp.bfloat16
    anywhere = pl.BlockSpec(memory_space=pltpu.HBM)
    vmem = pl.BlockSpec(memory_space=pltpu.VMEM)
    dma = pltpu.SemaphoreType.DMA
    norm_rows = n * m * piece // LANES
    hbm = lambda x: pltpu.with_memory_space_constraint(x, pltpu.HBM)
    blocks, *small = pl.pallas_call(
        gather_kernel,
        out_shape=(
            pltpu.VMEM((n * wide, cols), bf16),
            pltpu.VMEM((tiles, LANES), f32),
            pltpu.VMEM((1, thin), f32),
            pltpu.VMEM((1, thin), f32),
            pltpu.VMEM((norm_rows, LANES), bf16),
        ),
        in_specs=[anywhere] * 9,
        out_specs=(vmem,) * 5,
        scratch_shapes=[
            pltpu.VMEM((rows, cols), f32),
            pltpu.VMEM((rows, cols), f32),
            pltpu.VMEM((2 * thin, rows), f32),
            pltpu.VMEM((2 * thin, rows), f32),
            pltpu.VMEM((1, rows), f32),
            pltpu.VMEM((rows, LANES), f32),
            pltpu.VMEM((2, 1, piece), f32),
            pltpu.VMEM((8, LANES), f32),
            pltpu.VMEM((wide, cols), f32),
            pltpu.VMEM((n, tiles + 1, 1, LANES), f32),
            pltpu.VMEM((n, 1, LANES), f32),
            pltpu.VMEM((m, n, LANES), f32),
            pltpu.VMEM((norm_rows, LANES), f32),
            pltpu.VMEM((2, max(EARLY, 1) * wide // PIECES, cols), f32),
            dma((1 + 2 * tiles + 6,)),
            dma((4,)),
            dma((2 * (math.isqrt(m) - 1),)),
            dma((2 * (math.isqrt(m) - 1),)),
            dma((2 * max(EARLY, 1),)),
            dma((2 * max(EARLY, 1),)),
            dma((2,)),
            dma((n // 2 * PIECES,)),
            dma((n // 2 * PIECES,)),
        ],
        compiler_params=pltpu.CompilerParams(
            collective_id=0, has_side_effects=True, vmem_limit_bytes=24 * 1024 * 1024
        ),
        name="gather",
    )(
        hbm(first_q), hbm(second_q), hbm(first_k.T), hbm(second_k.T), hbm(first_v.T), hbm(second_v.T),
        hbm(mix.reshape(1, rows)), hbm(train.reshape(1, piece)), hbm(step.reshape(1, piece)),
    )
    query, key, value, f_query, f_key, f_value, norm = pl.pallas_call(
        functools.partial(place_kernel, n, rows, thin),
        out_shape=(
            jax.ShapeDtypeStruct((n * rows, cols), bf16),
            jax.ShapeDtypeStruct((thin, n * rows), bf16),
            jax.ShapeDtypeStruct((thin, n * rows), bf16),
            jax.ShapeDtypeStruct((tiles, LANES), f32),
            jax.ShapeDtypeStruct((1, thin), f32),
            jax.ShapeDtypeStruct((1, thin), f32),
            jax.ShapeDtypeStruct((norm_rows, LANES), bf16),
        ),
        in_specs=[vmem] * 5,
        out_specs=(anywhere,) * 7,
        scratch_shapes=[dma((3 * n + 4,))],
        compiler_params=pltpu.CompilerParams(vmem_limit_bytes=24 * 1024 * 1024),
        name="place",
    )(blocks, *small)
    return (
        query, key.T, value.T,
        f_query.reshape(-1), f_key.reshape(-1), f_value.reshape(-1), norm.reshape(-1),
    )


def solution(mesh):
    own = P(("unit", "zero"), "model")
    return jax.shard_map(
        on_device,
        mesh=mesh,
        in_specs=(own, own, own, own, own, own, P(("unit", "zero")), P(("unit", "zero", "model")), P(("unit", "zero", "model"))),
        out_specs=(
            P("unit", "model"), P("unit", "model"), P("unit", "model"),
            P(("unit", "model")), P(("unit", "model")), P(("unit", "model")), P("unit"),
        ),
        check_vma=False,
    )
```

time: 146 us -> 133 us (0.911)
  local copies, waits for them, and re-layouts: 8.05 us -> 0 us
  Pallas kernels: 137 us -> 131 us
    unnamed x18 -> x0, local copies, waits for them, and re-layouts: 8.05 us -> none
    pallas_call x1, Pallas kernels: 132 us -> 127 us  [on_device(): pl.pallas_call(gather_kernel, out_shape=(pltpu.VMEM((n * wide, cols), bf1...]
where the time goes in v2:
time: 133 us; the launch traced here: 132 us
  Pallas kernels  131 us (98%)
    pallas_call x1, Pallas kernels, on_device(): pl.pallas_call(gather_kernel, out_shape=(pltpu.VMEM((n * wide, cols), bf1...  127 us
    pallas_call x1, Pallas kernels, on_device(): pl.pallas_call(functools.partial(place_kernel, n, rows, thin), out_shape=...  4.35 us

profile of v2, /device:TPU:1, one launch (start us, length us, event | category | flops | bytes accessed | tf_op | source)
XLA Modules:
  0.0 131.9 jit_solution(5462926859642912873)
XLA Ops:
  0.6 126.9 %gather.1 = (bf16[10240,512]{1,0:T(8,128)(2,1)S(1)}, f32[4,128]{1,0:T(4,128)S(1)}, f32[1,64]{1,0:T(1,128)S(1)}, f32[1,64]{1,0:T(1,128)S(1)}, bf16[64,128]{1,0:T(8,128)(2,1)S(1)}) custom-call(f32[512,512]{1,0:T(8,128)} %first_q.1, f32[512,512]{1,0:T(8,128)} %second_q.1, f32[64,512]{1,0:T(8,128)} %bitcast.13, f32[64,512]{1,0:T(8,128)} %bitcast.14, ...), custom_call_target="tpu_custom_call" | custom-call | tf_op jit(solution)/shard_map/gather/pallas_call | solution.py:343
  127.5 4.3 %place.1 = (bf16[8192,512]{1,0:T(8,128)(2,1)}, bf16[64,8192]{1,0:T(8,128)(2,1)}, bf16[64,8192]{1,0:T(8,128)(2,1)}, f32[4,128]{1,0:T(4,128)}, f32[1,64]{1,0:T(1,1...) custom-call(bf16[10240,512]{1,0:T(8,128)(2,1)S(1)} %get-tuple-element.19.blocks, f32[4,128]{1,0:T(4,128)S(1)} %get-tuple-element.20.refs_0_, ...), custom_call_target="tpu_custom_call" | custom-call | tf_op jit(solution)/shard_map/place/pallas_call | solution.py:387

commit v3 on v2

--- a/solution.py
+++ b/solution.py
@@ -10,8 +10,8 @@
 
 MESH = pl.DeviceIdType.MESH
 LANES = 128
-PIECES = 8
-EARLY = 1
+PIECES = 4
+EARLY = 80
 
 
 def gather_kernel(
@@ -37,45 +37,65 @@
     def below(d):
         return lax.rem(down + d, side) * side + across
 
-    loads = [pltpu.make_async_copy(mix, mix_row, load_sem.at[0])]
+    def load(k, src, dst):
+        return pltpu.make_async_copy(src, dst, load_sem.at[k])
+
+    load_mix = load(0, mix, mix_row)
+    load_thin = [
+        load(1, first_k, a_kv.at[pl.ds(0, thin)]),
+        load(2, second_k, b_kv.at[pl.ds(0, thin)]),
+        load(3, first_v, a_kv.at[pl.ds(thin, thin)]),
+        load(4, second_v, b_kv.at[pl.ds(thin, thin)]),
+    ]
+    load_gain = [load(5, train, norm_in.at[0]), load(6, step, norm_in.at[1])]
+    load_q = []
     for r in range(tiles):
         part = pl.ds(r * LANES, LANES)
-        loads.append(pltpu.make_async_copy(first_q.at[part], a_q.at[part], load_sem.at[1 + 2 * r]))
-        loads.append(pltpu.make_async_copy(second_q.at[part], b_q.at[part], load_sem.at[2 + 2 * r]))
-    at = 1 + 2 * tiles
-    for k, (src, dst) in enumerate(
-        (
-            (first_k, a_kv.at[pl.ds(0, thin)]),
-            (first_v, a_kv.at[pl.ds(thin, thin)]),
-            (second_k, b_kv.at[pl.ds(0, thin)]),
-            (second_v, b_kv.at[pl.ds(thin, thin)]),
-            (train, norm_in.at[0]),
-            (step, norm_in.at[1]),
-        )
-    ):
-        loads.append(pltpu.make_async_copy(src, dst, load_sem.at[at + k]))
-    for load in loads:
-        load.start()
+        load_q.append(
+            (load(7 + 2 * r, first_q.at[part], a_q.at[part]), load(8 + 2 * r, second_q.at[part], b_q.at[part]))
+        )
+
+    def around(d):
+        return {"zero": lax.rem(me + d, n)}
 
     barrier = pltpu.get_barrier_semaphore()
 
-    def greet_line(d, c):
-        pl.semaphore_signal(barrier, inc=1, device_id={"zero": lax.rem(me + d, n)}, device_id_type=MESH)
-        return c
-
-    lax.fori_loop(1, n, greet_line, 0)
+    outward = [n // 2]
+    for d in range(n // 2 - 1, 0, -1):
+        outward += [d, n - d]
+    for d in outward:
+        pl.semaphore_signal(barrier, inc=1, device_id=around(d), device_id_type=MESH)
     for peer in (beside(1), beside(side - 1), below(1), below(side - 1)):
         pl.semaphore_signal(barrier, inc=1, device_id={"model": peer}, device_id_type=MESH)
-
-    loads[0].wait()
+    load_mix.start()
+    for copy in load_thin:
+        copy.start()
+    for pair in load_q:
+        for copy in pair:
+            copy.start()
+    for copy in load_gain:
+        copy.start()
+
+    load_mix.wait()
     for r in range(tiles):
         row = mix_row[:, r * LANES : (r + 1) * LANES]
         share[r * LANES : (r + 1) * LANES, :] = jnp.broadcast_to(row, (LANES, LANES)).T
 
     sums = [jnp.zeros((8, LANES), jnp.float32) for _ in range(tiles)]
     for r in range(tiles):
-        loads[1 + 2 * r].wait()
-        loads[2 + 2 * r].wait()
+        if r == tiles - 1:
+            for copy in load_thin:
+                copy.wait()
+            w = mix_row[...]
+            f = w * a_kv[...] + (1.0 - w) * b_kv[...]
+            fresh[rows:, :] = f
+            s = f * f
+            folded = s[:, :LANES]
+            for c in range(1, tiles):
+                folded = folded + s[:, c * LANES : (c + 1) * LANES]
+            stat[me, tiles] = jnp.sum(folded.T, axis=0, keepdims=True)
+        for copy in load_q[r]:
+            copy.wait()
         part = slice(r * LANES, (r + 1) * LANES)
         w = share[part, :]
         for c in range(tiles):
@@ -83,19 +103,41 @@
             f = w * a_q[part, lanes] + (1.0 - w) * b_q[part, lanes]
             fresh[part, lanes] = f
             sums[c] = sums[c] + jnp.sum((f * f).reshape(LANES // 8, 8, LANES), axis=0)
-    for load in loads[at : at + 4]:
-        load.wait()
-    w = mix_row[...]
-    f = w * a_kv[...] + (1.0 - w) * b_kv[...]
-    fresh[rows:, :] = f
-    s = f * f
-    folded = s[:, :LANES]
-    for c in range(1, tiles):
-        folded = folded + s[:, c * LANES : (c + 1) * LANES]
-    thin_sum = jnp.sum(folded.T, axis=0, keepdims=True)
-
-    for load in loads[at + 4 :]:
-        load.wait()
+    for c in range(tiles):
+        stat[me, c] = jnp.sum(sums[c], axis=0, keepdims=True)
+
+    pl.semaphore_wait(barrier, n - 1 + 4)
+
+    def to_line(ref, k, d):
+        return pltpu.make_async_remote_copy(
+            ref.at[me], ref.at[me], line_sem.at[2 * k], line_sem.at[2 * k + 1],
+            device_id=around(d), device_id_type=MESH,
+        )
+
+    def whole_line(ref, k):
+        every = ref.at[pl.ds(0, n - 1)]
+        return pltpu.make_async_remote_copy(
+            every, every, line_sem.at[2 * k], line_sem.at[2 * k + 1],
+            device_id={"zero": lax.rem(me + 1, n)}, device_id_type=MESH,
+        )
+
+    for d in outward:
+        to_line(stat, 0, d).start()
+
+    after, before = lax.rem(me + 1, n), lax.rem(me + n - 1, n)
+
+    def early_copy(way):
+        return pltpu.make_async_remote_copy(
+            fresh.at[pl.ds(0, EARLY)], early.at[way], early_send.at[way], early_recv.at[way],
+            device_id={"zero": (after, before)[way]}, device_id_type=MESH,
+        )
+
+    ways = (0, 1) if EARLY else ()
+    for way in ways:
+        early_copy(way).start()
+
+    for copy in load_gain:
+        copy.wait()
     gain = (norm_in[0] + norm_in[1]).astype(jnp.bfloat16).astype(jnp.float32)
     lane_row[...] = jnp.zeros_like(lane_row)
     share_of_row = gain.shape[1]
@@ -108,44 +150,9 @@
     lane = lax.broadcasted_iota(jnp.int32, (8, LANES), 1)
     spread = jnp.where(lane // share_of_row == lax.rem(col, per_row), spread, 0.0)
 
-    for c in range(tiles):
-        stat[me, c] = jnp.sum(sums[c], axis=0, keepdims=True)
-    stat[me, tiles] = thin_sum
     gains[me] = spread[0:1, :]
-
-    pl.semaphore_wait(barrier, n - 1 + 4)
-
-    def to_line(ref, k, d):
-        return pltpu.make_async_remote_copy(
-            ref.at[me], ref.at[me], line_sem.at[2 * k], line_sem.at[2 * k + 1],
-            device_id={"zero": lax.rem(me + d, n)}, device_id_type=MESH,
-        )
-
-    def whole_line(ref, k):
-        every = ref.at[pl.ds(0, n - 1)]
-        return pltpu.make_async_remote_copy(
-            every, every, line_sem.at[2 * k], line_sem.at[2 * k + 1],
-            device_id={"zero": lax.rem(me + 1, n)}, device_id_type=MESH,
-        )
-
-    for k, ref in enumerate((stat, gains)):
-        to_line(ref, k, n // 2).start()
-        for d in range(1, n // 2):
-            to_line(ref, k, n // 2 + d).start()
-            to_line(ref, k, n // 2 - d).start()
-
-    after, before = lax.rem(me + 1, n), lax.rem(me + n - 1, n)
-
-    def early_copy(p, way):
-        where = pl.ds(p * size, size)
-        return pltpu.make_async_remote_copy(
-            fresh.at[where], early.at[way, where], early_send.at[way * EARLY + p], early_recv.at[way * EARLY + p],
-            device_id={"zero": (after, before)[way]}, device_id_type=MESH,
-        )
-
-    for p in range(EARLY):
-        early_copy(p, 0).start()
-        early_copy(p, 1).start()
+    for d in outward:
+        to_line(gains, 1, d).start()
 
     whole_line(stat, 0).wait_recv()
 
@@ -163,9 +170,8 @@
             f_value[...] = factor[:, thin:]
     thin_inverse = jnp.broadcast_to(inverse[tiles], (LANES, LANES)).T
 
-    def rounded(source, owner, p):
+    def rounded(source, owner, low, high):
         base = pl.multiple_of(owner * wide, wide)
-        low, high = p * size, (p + 1) * size
         edge = min(max(rows, low), high)
         if low < edge:
             for c in range(tiles):
@@ -178,7 +184,9 @@
                 blocks[pl.ds(base + edge, high - edge), lanes] = (source[edge:high, lanes] * scale).astype(jnp.bfloat16)
 
     def piece_copy(way, recv, origin, s, p, to):
-        where = blocks.at[pl.ds(pl.multiple_of(origin * wide + p * size, size), size)]
+        skip = EARLY if s == 0 and p == 0 else 0
+        start = pl.multiple_of(origin * wide + p * size + skip, 16)
+        where = blocks.at[pl.ds(start, size - skip)]
         return pltpu.make_async_remote_copy(
             where, where, sent_sem.at[way], recv.at[s * PIECES + p],
             device_id={"zero": to}, device_id_type=MESH,
@@ -196,31 +204,22 @@
     def from_right(s, p):
         return piece_copy(1, left_recv, lax.rem(after + s, n), s, p, before)
 
-    def both(s, p):
-        to_right(s, p).start()
-        to_left(s, p).start()
-
-    for p in range(EARLY, PIECES):
-        rounded(fresh, me, p)
-        if p > EARLY:
-            both(0, p - 1)
-    for p in range(EARLY):
-        rounded(fresh, me, p)
-    both(0, PIECES - 1)
-    for p in range(EARLY):
-        early_copy(p, 0).wait_recv()
-        rounded(early.at[0], before, p)
+    for p in range(PIECES):
+        rounded(fresh, me, p * size if p else EARLY, (p + 1) * size)
         if p:
-            to_left(1, p - 1).start()
-        early_copy(p, 1).wait_recv()
-        rounded(early.at[1], after, p)
-        to_right(1, p).start()
+            to_right(0, p - 1).start()
+            to_left(0, p - 1).start()
+    if EARLY:
+        rounded(fresh, me, 0, EARLY)
+    to_right(0, PIECES - 1).start()
+    to_left(0, PIECES - 1).start()
+    for way in ways:
+        early_copy(way).wait_recv()
+        rounded(early.at[way], (before, after)[way], 0, EARLY)
 
     whole_line(gains, 1).wait_recv()
     for z in range(n):
         plane[col, z : z + 1, :] = gains[z]
-    if EARLY:
-        to_left(1, EARLY - 1).start()
 
     def plane_copy(k):
         if k < side - 1:
@@ -256,7 +255,8 @@
             to_left(s, p).start()
             return c
 
-        lax.fori_loop(EARLY if s == 1 else 0, PIECES, one, 0)
+        for p in range(PIECES):
+            one(p, 0)
         if s <= turns:
             plane_from(s - 1).wait_recv()
             if s < turns:
@@ -295,10 +295,9 @@
     lax.fori_loop(0, half, far, 0)
     lax.fori_loop(0, half, end, 0)
 
-    for p in range(EARLY):
-        early_copy(p, 0).wait_send()
-        early_copy(p, 1).wait_send()
-    out = blocks.at[pl.ds(0, (last * PIECES - EARLY + half) * size)]
+    for way in ways:
+        early_copy(way).wait_send()
+    out = blocks.at[pl.ds(0, (last * PIECES + half) * size - EARLY)]
     for way, to in enumerate((after, before)):
         pltpu.make_async_remote_copy(
             out, out, sent_sem.at[way], right_recv.at[0], device_id={"zero": to}, device_id_type=MESH
@@ -313,18 +312,20 @@
     query, key, value = refs[4:7]
     sems = refs[-1]
     wide = rows + 2 * thin
-    pairs = []
     for z in range(n):
         here = pl.ds(z * rows, rows)
-        pairs.append((blocks.at[pl.ds(z * wide, rows)], query.at[here]))
-        pairs.append((blocks.at[pl.ds(z * wide + rows, thin)], key.at[:, here]))
-        pairs.append((blocks.at[pl.ds(z * wide + rows + thin, thin)], value.at[:, here]))
-    pairs.extend(zip(refs[:4], refs[7:11]))
-    copies = [pltpu.make_async_copy(src, dst, sems.at[k]) for k, (src, dst) in enumerate(pairs)]
-    for copy in copies:
+        pltpu.make_async_copy(blocks.at[pl.ds(z * wide, rows)], query.at[here], sems.at[0]).start()
+        pltpu.make_async_copy(blocks.at[pl.ds(z * wide + rows, thin)], key.at[:, here], sems.at[1]).start()
+        pltpu.make_async_copy(blocks.at[pl.ds(z * wide + rows + thin, thin)], value.at[:, here], sems.at[2]).start()
+    small = [
+        pltpu.make_async_copy(src, dst, sems.at[3 + k]) for k, (src, dst) in enumerate(zip(refs[:4], refs[7:11]))
+    ]
+    for copy in small:
         copy.start()
-    for copy in copies:
+    for copy in small:
         copy.wait()
+    for k, large in enumerate((query, key, value)):
+        pltpu.make_async_copy(large, large, sems.at[k]).wait()
 
 
 def on_device(first_q, second_q, first_k, second_k, first_v, second_v, mix, train, step):
@@ -365,13 +366,13 @@
             pltpu.VMEM((n, 1, LANES), f32),
             pltpu.VMEM((m, n, LANES), f32),
             pltpu.VMEM((norm_rows, LANES), f32),
-            pltpu.VMEM((2, max(EARLY, 1) * wide // PIECES, cols), f32),
-            dma((1 + 2 * tiles + 6,)),
+            pltpu.VMEM((2, max(EARLY, 8), cols), f32),
+            dma((7 + 2 * tiles,)),
             dma((4,)),
             dma((2 * (math.isqrt(m) - 1),)),
             dma((2 * (math.isqrt(m) - 1),)),
-            dma((2 * max(EARLY, 1),)),
-            dma((2 * max(EARLY, 1),)),
+            dma((2,)),
+            dma((2,)),
             dma((2,)),
             dma((n // 2 * PIECES,)),
             dma((n // 2 * PIECES,)),
@@ -397,7 +398,7 @@
         ),
         in_specs=[vmem] * 5,
         out_specs=(anywhere,) * 7,
-        scratch_shapes=[dma((3 * n + 4,))],
+        scratch_shapes=[dma((7,))],
         compiler_params=pltpu.CompilerParams(vmem_limit_bytes=24 * 1024 * 1024),
         name="place",
     )(blocks, *small)

time: 133 us -> 132 us (level)
  no operation moved by 1% of the time
where the time goes in v3:
time: 132 us; the launch traced here: 131 us
  Pallas kernels  130 us (98%)
    pallas_call x1, Pallas kernels, on_device(): pl.pallas_call(gather_kernel, out_shape=(pltpu.VMEM((n * wide, cols), bf1...  126 us
    pallas_call x1, Pallas kernels, on_device(): pl.pallas_call(functools.partial(place_kernel, n, rows, thin), out_shape=...  3.95 us

profile of v3, /device:TPU:1, one launch (start us, length us, event | category | flops | bytes accessed | tf_op | source)
XLA Modules:
  0.0 130.6 jit_solution(12973652920966802908)
XLA Ops:
  0.6 126.0 %gather.1 = (bf16[10240,512]{1,0:T(8,128)(2,1)S(1)}, f32[4,128]{1,0:T(4,128)S(1)}, f32[1,64]{1,0:T(1,128)S(1)}, f32[1,64]{1,0:T(1,128)S(1)}, bf16[64,128]{1,0:T(8,128)(2,1)S(1)}) custom-call(f32[512,512]{1,0:T(8,128)} %first_q.1, f32[512,512]{1,0:T(8,128)} %second_q.1, f32[64,512]{1,0:T(8,128)} %bitcast.13, f32[64,512]{1,0:T(8,128)} %bitcast.14, ...), custom_call_target="tpu_custom_call" | custom-call | tf_op jit(solution)/shard_map/gather/pallas_call | solution.py:344
  126.7 4.0 %place.1 = (bf16[8192,512]{1,0:T(8,128)(2,1)}, bf16[64,8192]{1,0:T(8,128)(2,1)}, bf16[64,8192]{1,0:T(8,128)(2,1)}, f32[4,128]{1,0:T(4,128)}, f32[1,64]{1,0:T(1,1...) custom-call(bf16[10240,512]{1,0:T(8,128)(2,1)S(1)} %get-tuple-element.19.blocks, f32[4,128]{1,0:T(4,128)S(1)} %get-tuple-element.20.refs_0_, ...), custom_call_target="tpu_custom_call" | custom-call | tf_op jit(solution)/shard_map/place/pallas_call | solution.py:388

commit v4 on v3

--- a/solution.py
+++ b/solution.py
@@ -11,13 +11,13 @@
 MESH = pl.DeviceIdType.MESH
 LANES = 128
 PIECES = 4
-EARLY = 80
+EARLY = 96
 
 
 def gather_kernel(
     first_q, second_q, first_k, second_k, first_v, second_v, mix, train, step,
     blocks, f_query, f_key, f_value, norm,
-    a_q, b_q, a_kv, b_kv, mix_row, share, norm_in, lane_row, fresh, stat, gains, plane, norm_wide, early,
+    a_q, b_q, a_kv, b_kv, mix_row, share, norm_in, lane_row, fresh, stat, plane, norm_wide, early,
     load_sem, line_sem, plane_send, plane_recv, early_send, early_recv, sent_sem, right_recv, left_recv,
 ):
     n, m = lax.axis_size("zero"), lax.axis_size("model")
@@ -106,36 +106,6 @@
     for c in range(tiles):
         stat[me, c] = jnp.sum(sums[c], axis=0, keepdims=True)
 
-    pl.semaphore_wait(barrier, n - 1 + 4)
-
-    def to_line(ref, k, d):
-        return pltpu.make_async_remote_copy(
-            ref.at[me], ref.at[me], line_sem.at[2 * k], line_sem.at[2 * k + 1],
-            device_id=around(d), device_id_type=MESH,
-        )
-
-    def whole_line(ref, k):
-        every = ref.at[pl.ds(0, n - 1)]
-        return pltpu.make_async_remote_copy(
-            every, every, line_sem.at[2 * k], line_sem.at[2 * k + 1],
-            device_id={"zero": lax.rem(me + 1, n)}, device_id_type=MESH,
-        )
-
-    for d in outward:
-        to_line(stat, 0, d).start()
-
-    after, before = lax.rem(me + 1, n), lax.rem(me + n - 1, n)
-
-    def early_copy(way):
-        return pltpu.make_async_remote_copy(
-            fresh.at[pl.ds(0, EARLY)], early.at[way], early_send.at[way], early_recv.at[way],
-            device_id={"zero": (after, before)[way]}, device_id_type=MESH,
-        )
-
-    ways = (0, 1) if EARLY else ()
-    for way in ways:
-        early_copy(way).start()
-
     for copy in load_gain:
         copy.wait()
     gain = (norm_in[0] + norm_in[1]).astype(jnp.bfloat16).astype(jnp.float32)
@@ -150,11 +120,37 @@
     lane = lax.broadcasted_iota(jnp.int32, (8, LANES), 1)
     spread = jnp.where(lane // share_of_row == lax.rem(col, per_row), spread, 0.0)
 
-    gains[me] = spread[0:1, :]
+    stat[me, tiles + 1] = spread[0:1, :]
+
+    pl.semaphore_wait(barrier, n - 1 + 4)
+
+    def to_line(d):
+        return pltpu.make_async_remote_copy(
+            stat.at[me], stat.at[me], line_sem.at[0], line_sem.at[1], device_id=around(d), device_id_type=MESH
+        )
+
+    def whole_line():
+        every = stat.at[pl.ds(0, n - 1)]
+        return pltpu.make_async_remote_copy(
+            every, every, line_sem.at[0], line_sem.at[1], device_id=around(1), device_id_type=MESH
+        )
+
     for d in outward:
-        to_line(gains, 1, d).start()
-
-    whole_line(stat, 0).wait_recv()
+        to_line(d).start()
+
+    after, before = lax.rem(me + 1, n), lax.rem(me + n - 1, n)
+
+    def early_copy(way):
+        return pltpu.make_async_remote_copy(
+            fresh.at[pl.ds(0, EARLY)], early.at[way], early_send.at[way], early_recv.at[way],
+            device_id={"zero": (after, before)[way]}, device_id_type=MESH,
+        )
+
+    ways = (0, 1) if EARLY else ()
+    for way in ways:
+        early_copy(way).start()
+
+    whole_line().wait_recv()
 
     inverse = []
     for c in range(tiles + 1):
@@ -217,9 +213,8 @@
         early_copy(way).wait_recv()
         rounded(early.at[way], (before, after)[way], 0, EARLY)
 
-    whole_line(gains, 1).wait_recv()
     for z in range(n):
-        plane[col, z : z + 1, :] = gains[z]
+        plane[col, z : z + 1, :] = stat[z, tiles + 1]
 
     def plane_copy(k):
         if k < side - 1:
@@ -302,8 +297,7 @@
         pltpu.make_async_remote_copy(
             out, out, sent_sem.at[way], right_recv.at[0], device_id={"zero": to}, device_id_type=MESH
         ).wait_send()
-    whole_line(stat, 0).wait_send()
-    whole_line(gains, 1).wait_send()
+    whole_line().wait_send()
     for k in range(turns):
         plane_copy(k).wait_send()
 
@@ -362,13 +356,12 @@
             pltpu.VMEM((2, 1, piece), f32),
             pltpu.VMEM((8, LANES), f32),
             pltpu.VMEM((wide, cols), f32),
-            pltpu.VMEM((n, tiles + 1, 1, LANES), f32),
-            pltpu.VMEM((n, 1, LANES), f32),
+            pltpu.VMEM((n, tiles + 2, 1, LANES), f32),
             pltpu.VMEM((m, n, LANES), f32),
             pltpu.VMEM((norm_rows, LANES), f32),
             pltpu.VMEM((2, max(EARLY, 8), cols), f32),
             dma((7 + 2 * tiles,)),
-            dma((4,)),
+            dma((2,)),
             dma((2 * (math.isqrt(m) - 1),)),
             dma((2 * (math.isqrt(m) - 1),)),
             dma((2,)),

time: 132 us -> 131 us (level); the launches traced: 131 us -> 131 us
  no operation moved by 1% of the time
where the time goes in v4:
time: 131 us
  Pallas kernels  131 us (100%)
    pallas_call x1, Pallas kernels, on_device(): pl.pallas_call(gather_kernel, out_shape=(pltpu.VMEM((n * wide, cols), bf1...  127 us
    pallas_call x1, Pallas kernels, on_device(): pl.pallas_call(functools.partial(place_kernel, n, rows, thin), out_shape=...  3.95 us

profile of v4, /device:TPU:1, one launch (start us, length us, event | category | flops | bytes accessed | tf_op | source)
XLA Modules:
  0.0 131.3 jit_solution(8722262183910447902)
XLA Ops:
  0.6 126.7 %gather.1 = (bf16[10240,512]{1,0:T(8,128)(2,1)S(1)}, f32[4,128]{1,0:T(4,128)S(1)}, f32[1,64]{1,0:T(1,128)S(1)}, f32[1,64]{1,0:T(1,128)S(1)}, bf16[64,128]{1,0:T(8,128)(2,1)S(1)}) custom-call(f32[512,512]{1,0:T(8,128)} %first_q.1, f32[512,512]{1,0:T(8,128)} %second_q.1, f32[64,512]{1,0:T(8,128)} %bitcast.13, f32[64,512]{1,0:T(8,128)} %bitcast.14, ...), custom_call_target="tpu_custom_call" | custom-call | tf_op jit(solution)/shard_map/gather/pallas_call | solution.py:338
  127.3 4.0 %place.1 = (bf16[8192,512]{1,0:T(8,128)(2,1)}, bf16[64,8192]{1,0:T(8,128)(2,1)}, bf16[64,8192]{1,0:T(8,128)(2,1)}, f32[4,128]{1,0:T(4,128)}, f32[1,64]{1,0:T(1,1...) custom-call(bf16[10240,512]{1,0:T(8,128)(2,1)S(1)} %get-tuple-element.19.blocks, f32[4,128]{1,0:T(4,128)S(1)} %get-tuple-element.20.refs_0_, ...), custom_call_target="tpu_custom_call" | custom-call | tf_op jit(solution)/shard_map/place/pallas_call | solution.py:381

commit v5 on v4

--- a/solution.py
+++ b/solution.py
@@ -65,7 +65,7 @@
         outward += [d, n - d]
     for d in outward:
         pl.semaphore_signal(barrier, inc=1, device_id=around(d), device_id_type=MESH)
-    for peer in (beside(1), beside(side - 1), below(1), below(side - 1)):
+    for peer in (beside(side - 1), below(side - 1)):
         pl.semaphore_signal(barrier, inc=1, device_id={"model": peer}, device_id_type=MESH)
     load_mix.start()
     for copy in load_thin:
@@ -122,7 +122,7 @@
 
     stat[me, tiles + 1] = spread[0:1, :]
 
-    pl.semaphore_wait(barrier, n - 1 + 4)
+    pl.semaphore_wait(barrier, n - 1 + 2)
 
     def to_line(d):
         return pltpu.make_async_remote_copy(
@@ -152,19 +152,14 @@
 
     whole_line().wait_recv()
 
-    inverse = []
-    for c in range(tiles + 1):
+    def factor_of(c):
         total = stat[0, c]
         for z in range(1, n):
             total = total + stat[z, c]
-        factor = jnp.sqrt(total)
-        inverse.append(1.0 / factor)
-        if c < tiles:
-            f_query[c : c + 1, :] = factor
-        else:
-            f_key[...] = factor[:, :thin]
-            f_value[...] = factor[:, thin:]
-    thin_inverse = jnp.broadcast_to(inverse[tiles], (LANES, LANES)).T
+        return jnp.sqrt(total)
+
+    factor = [factor_of(c) for c in range(tiles)]
+    inverse = [1.0 / f for f in factor]
 
     def rounded(source, owner, low, high):
         base = pl.multiple_of(owner * wide, wide)
@@ -174,7 +169,7 @@
                 lanes = slice(c * LANES, (c + 1) * LANES)
                 blocks[pl.ds(base + low, edge - low), lanes] = (source[low:edge, lanes] * inverse[c]).astype(jnp.bfloat16)
         if edge < high:
-            scale = thin_inverse[edge - rows : high - rows, :]
+            scale = thin_inverse[0][edge - rows : high - rows, :]
             for c in range(tiles):
                 lanes = slice(c * LANES, (c + 1) * LANES)
                 blocks[pl.ds(base + edge, high - edge), lanes] = (source[edge:high, lanes] * scale).astype(jnp.bfloat16)
@@ -200,9 +195,19 @@
     def from_right(s, p):
         return piece_copy(1, left_recv, lax.rem(after + s, n), s, p, before)
 
+    thin_inverse = []
     for p in range(PIECES):
         rounded(fresh, me, p * size if p else EARLY, (p + 1) * size)
-        if p:
+        if p == 0:
+            thin_factor = factor_of(tiles)
+            thin_inverse.append(jnp.broadcast_to(1.0 / thin_factor, (LANES, LANES)).T)
+            for c in range(tiles):
+                f_query[c : c + 1, :] = factor[c]
+            f_key[...] = thin_factor[:, :thin]
+            f_value[...] = thin_factor[:, thin:]
+            to_right(0, 0).start()
+            to_left(0, 0).start()
+        if p > 1:
             to_right(0, p - 1).start()
             to_left(0, p - 1).start()
     if EARLY:

time: 131 us -> 131 us (level)
  no operation moved by 1% of the time
where the time goes in v5:
time: 131 us
  Pallas kernels  131 us (100%)
    pallas_call x1, Pallas kernels, on_device(): pl.pallas_call(gather_kernel, out_shape=(pltpu.VMEM((n * wide, cols), bf1...  127 us
    pallas_call x1, Pallas kernels, on_device(): pl.pallas_call(functools.partial(place_kernel, n, rows, thin), out_shape=...  3.95 us

profile of v5, /device:TPU:1, one launch (start us, length us, event | category | flops | bytes accessed | tf_op | source)
XLA Modules:
  0.0 131.3 jit_solution(13321815376580411207)
XLA Ops:
  0.6 126.7 %gather.1 = (bf16[10240,512]{1,0:T(8,128)(2,1)S(1)}, f32[4,128]{1,0:T(4,128)S(1)}, f32[1,64]{1,0:T(1,128)S(1)}, f32[1,64]{1,0:T(1,128)S(1)}, bf16[64,128]{1,0:T(8,128)(2,1)S(1)}) custom-call(f32[512,512]{1,0:T(8,128)} %first_q.1, f32[512,512]{1,0:T(8,128)} %second_q.1, f32[64,512]{1,0:T(8,128)} %bitcast.13, f32[64,512]{1,0:T(8,128)} %bitcast.14, ...), custom_call_target="tpu_custom_call" | custom-call | tf_op jit(solution)/shard_map/gather/pallas_call | solution.py:343
  127.3 4.0 %place.1 = (bf16[8192,512]{1,0:T(8,128)(2,1)}, bf16[64,8192]{1,0:T(8,128)(2,1)}, bf16[64,8192]{1,0:T(8,128)(2,1)}, f32[4,128]{1,0:T(4,128)}, f32[1,64]{1,0:T(1,1...) custom-call(bf16[10240,512]{1,0:T(8,128)(2,1)S(1)} %get-tuple-element.19.blocks, f32[4,128]{1,0:T(4,128)S(1)} %get-tuple-element.20.refs_0_, ...), custom_call_target="tpu_custom_call" | custom-call | tf_op jit(solution)/shard_map/place/pallas_call | solution.py:386
